TPU v7x, 32 devices: a whole 2x2x4 slice. The times are simulated.
32 devices in a mesh: dev: 32 (over z, y, x, core).
Axes of the slice: x: 2, y: 2, z: 4, core: 2. Of those that a mesh axis runs over, the one named last changes fastest.
Arguments:
- pixels: bfloat16 [96, 64, 16], P('dev'), may hold values from -6 to 6
- embed_w: bfloat16 [96, 16, 8192], P('dev'), may hold values from -1.5 to 1.5
- var_embed: bfloat16 [96, 8192], P('dev'), may hold values from -3 to 3
- key_w: bfloat16 [8192, 8192], P('dev'), may hold values from -0.0625 to 0.0625
- query: float32 [8192], replicated, may hold values from -500 to 500
- value_t: bfloat16 [8192, 8192], P('dev'), may hold values from -0.0625 to 0.0625
- out_w: bfloat16 [8192, 8192], P('dev'), may hold values from -0.0625 to 0.0625
Outputs:
- mixed: bfloat16 [64, 8192], P('dev')
All inputs are finite; a program needn't handle non-finite values.
Results may differ from a plain program's by a relative error of at most 0.012.
The roundings to bfloat16 on the way count: a program that leaves them out, or rounds other values in their place, can miss the bound.
Values may be sent and summed in bfloat16 or wider, within the bound.
A program may use at most 64 MiB of HBM per device.

v0:
```python
import jax
import jax.numpy as jnp
from jax import lax
from jax.sharding import PartitionSpec as P

D = 8192
HEADS = 64
HD = 128
V = 91


def body(pixels, embed_w, var_embed, key_w, query, value_t, out_w):
    group_size = lax.axis_size("dev")
    own_embed = jnp.einsum("vtp,vpd->vtd", pixels, embed_w, preferred_element_type=jnp.float32)
    own_embed = (own_embed + var_embed.astype(jnp.float32)[:, None, :]).astype(jnp.bfloat16)
    grouped = lax.all_to_all(own_embed, "dev", split_axis=1, concat_axis=0, tiled=True)
    key_rows = key_w.shape[0]
    keyq_part = jnp.einsum(
        "dhj,hj->dh",
        key_w.astype(jnp.float32).reshape(key_rows, HEADS, HD),
        query.reshape(HEADS, HD),
        precision=lax.Precision.HIGHEST,
    )
    keyq = lax.all_gather(keyq_part, "dev", axis=0, tiled=True)
    logits = jnp.einsum(
        "vtd,dh->vth", grouped.astype(jnp.float32), keyq, precision=lax.Precision.HIGHEST
    ) / jnp.sqrt(jnp.float32(HD))
    slot = lax.broadcasted_iota(jnp.int32, logits.shape, 0)
    logits = jnp.where(slot < V, logits, -1e30)
    row_max = jnp.max(logits, axis=0, keepdims=True)
    weights = jnp.exp(logits - row_max)
    attn = (weights / jnp.sum(weights, axis=0, keepdims=True)).astype(jnp.bfloat16)
    pooled = jnp.einsum("vth,vtd->thd", attn, grouped, preferred_element_type=jnp.float32).astype(
        jnp.bfloat16
    )
    own_tokens = pooled.shape[0]
    if group_size >= HEADS:
        spread = jnp.repeat(pooled, group_size // HEADS, axis=1)[:, :, None, :]
    else:
        spread = pooled.reshape(own_tokens, group_size, HEADS // group_size, D)
    received = lax.all_to_all(spread, "dev", split_axis=1, concat_axis=0, tiled=True)
    all_tokens = received.shape[0]
    head_share = received.shape[2]
    received = received.reshape(all_tokens, head_share, D)
    columns = value_t.shape[0]
    value_heads = jnp.einsum(
        "thd,hcd->thc",
        received,
        value_t.reshape(head_share, columns // head_share, D),
        preferred_element_type=jnp.float32,
    )
    value_heads = value_heads.reshape(all_tokens, columns).astype(jnp.bfloat16)
    summed = lax.psum_scatter(
        jnp.dot(value_heads, out_w, preferred_element_type=jnp.float32),
        "dev",
        scatter_dimension=0,
        tiled=True,
    )
    return summed.astype(jnp.bfloat16)


def solution(mesh):
    placed = (
        P("dev", None, None),
        P("dev", None, None),
        P("dev", None),
        P("dev", None),
        P(),
        P("dev", None),
        P("dev", None),
    )
    return jax.shard_map(
        body, mesh=mesh, in_specs=placed, out_specs=P("dev", None), check_vma=False
    )
```

profile of v0, /device:TPU:0, one launch (start us, length us, event | category | flops | bytes accessed | tf_op | source)
XLA Modules:
  0.0 285.6 jit_solution(11926075932730230169)
XLA Ops:
  6.5 0.0 copy-start
  6.5 0.9 convert_element_type.26
  7.5 0.2 copy-done
  7.7 1.7 fusion.1
  9.4 4.7 %copy.15 = bf16[3,64,8192]{2,0,1:T(4,128)(2,1)} copy(bf16[3,64,8192]{2,1,0:T(8,128)(2,1)S(1)} %fusion.1) | data formatting | bytes 6291456 | tf_op jit(solution)/shard_map/convert_element_type | solution.py:15
  14.1 7.4 %all-to-all-start = ((bf16[3,64,8192]{2,0,1:T(4,128)(2,1)}), bf16[3,64,8192]{2,0,1:T(4,128)(2,1)}, u32[]{:S(2)}, u32[]{:S(2)}) async-start(bf16[3,64,8192]{2,0,1:T(4,128)(2,1)} %copy.15), calls=%async_computation | async-start | bytes 8388608 | tf_op jit(solution)/shard_map/all_to_all | solution.py:16
  21.6 0.0 copy-start.2
  21.6 0.0 all-gather.2.cloned.1.call-start
  21.6 6.4 %copy.25 = bf16[256,8192]{0,1:T(8,128)(2,1)} copy(bf16[256,8192]{1,0:T(8,128)(2,1)} %param.10) | data formatting | bytes 8388608 | tf_op jit(solution)/shard_map/reshape | solution.py:20
  28.0 0.0 copy-done.2
  28.0 3.9 %fusion.32 = f32[64,1,256]{2,1,0:T(1,128)S(1)} fusion(f32[64,128,1]{1,2,0:T(1,128)S(1)} %bitcast.48, bf16[256,64,128]{0,2,1:T(8,128)(2,1)} %bitcast.44), kind=kOutput, calls=%fused_computation.26 | convolution fusion | flops 25165824 | bytes 4292608 | tf_op jit(solution)/shard_map/dhj,hj->dh/dot_general | solution.py:18
  31.9 0.6 copy.47
  32.5 0.0 all-gather.2.cloned.1.call-update
  32.6 93.2 %all-to-all-done = bf16[3,64,8192]{2,0,1:T(4,128)(2,1)} async-done(((bf16[3,64,8192]{2,0,1:T(4,128)(2,1)}), bf16[3,64,8192]{2,0,1:T(4,128)(2,1)}, u32[]{:S(2)}, u32[]{:S(2)}) %all-to-all-start) | async-done | bytes 3145760 | tf_op jit(solution)/shard_map/all_to_all | solution.py:16
  125.8 7.9 %copy.16 = bf16[3,32,2,8192]{3,2,0,1:T(2,128)(2,1)} copy(bf16[3,32,2,8192]{3,0,2,1:T(4,128)(2,1)} %bitcast) | data formatting | bytes 6291456 | tf_op jit(solution)/shard_map/all_to_all | solution.py:16
  133.7 0.0 all-gather.2.cloned.1.call-done
  133.7 9.0 %fusion.15 = f32[96,2,64]{0,2,1:T(8,128)S(1)} fusion(f32[8192,64]{0,1:T(8,128)} %all-gather.2.cloned.1.call-done, bf16[96,2,8192]{2,1,0:T(2,128)(2,1)} %bitcast.42, pred[96]{0:T(512)(128)(4,1)S(1)} %iota_compare_fusion), kind=kOutput, calls=%fused_computation.13 | convolution fusion | flops 1207984128 | bytes 5292128 | tf_op jit(solution)/shard_map/vtd,dh->vth/dot_general | solution.py:25
  142.7 0.2 fusion.31
  142.9 6.0 %convolution_convert_fusion = bf16[2,64,8192]{2,1,0:T(8,128)(2,1)S(1)} fusion(bf16[96,2,8192]{2,1,0:T(2,128)(2,1)} %bitcast.43, f32[2,64]{1,0:T(2,128)S(1)} %fusion.31, f32[96,2,64]{0,2,1:T(8,128)S(1)} %fusion.15), kind=kOutput, calls=%fused_computation.3 | convolution fusion | flops 202412256 | bytes 5292544 | tf_op jit(solution)/shard_map/vth,vtd->thd/dot_general | solution.py:33
  148.9 2.7 reshape.23
  151.6 6.0 %copy.19 = bf16[2,32,2,8192]{3,2,0,1:T(2,128)(2,1)} copy(bf16[2,32,2,8192]{3,2,1,0:T(2,128)(2,1)} %reshape.23) | data formatting | bytes 4194304 | tf_op jit(solution)/shard_map/reshape | solution.py:40
  157.5 4.1 %all-to-all-start.1 = ((bf16[2,32,2,8192]{3,2,0,1:T(2,128)(2,1)}), bf16[2,32,2,8192]{3,2,0,1:T(2,128)(2,1)S(1)}, u32[]{:S(2)}, u32[]{:S(2)}) async-start(bf16[2,32,2,8192]{3,2,0,1:T(2,128)(2,1)} %copy.19), calls=%async_computation.1 | async-start | bytes 4194304 | tf_op jit(solution)/shard_map/all_to_all | solution.py:41
  161.7 48.7 %all-to-all-done.1 = bf16[2,32,2,8192]{3,2,0,1:T(2,128)(2,1)S(1)} async-done(((bf16[2,32,2,8192]{3,2,0,1:T(2,128)(2,1)}), bf16[2,32,2,8192]{3,2,0,1:T(2,128)(2,1)S(1)}, u32[]{:S(2)}, u32[]{:S(2)}) %all-to-all-start.1) | async-done | bytes 2097184 | tf_op jit(solution)/shard_map/all_to_all | solution.py:41
  210.4 0.0 copy-start.1
  210.4 4.1 %fusion.23 = bf16[2,8,8,128]{3,2,1,0:T(8,128)(2,1)S(1)} fusion(bf16[2,128,8192]{2,1,0:T(8,128)(2,1)} %bitcast.46, bf16[64,2,8192]{2,1,0:T(2,128)(2,1)S(1)} %bitcast.45), kind=kOutput, calls=%fused_computation.15 | convolution fusion | flops 268451840 | bytes 6324224 | tf_op jit(solution)/shard_map/thd,hcd->thc/dot_general | solution.py:46
  214.5 0.0 copy-done.1
  214.5 0.8 fusion.26
  215.4 61.8 %all-reduce.2 = bf16[64,8192]{1,0:T(8,128)(2,1)} all-reduce(f32[64,8192]{1,0:T(8,128)S(1)} %fusion.26), channel_id=2, replica_groups=mesh['dev'=32] {'dev'}, use_global_device_ids=true, to_apply=%region_2.3.clone | all-reduce | flops 524288 | bytes 3145728
  277.2 1.6 dynamic-slice_convert_fusion
  (1 shorter events, 0.0 us)
Async XLA Ops:
  6.5 1.2 copy-start
  14.1 111.7 %all-to-all-start = ((bf16[3,64,8192]{2,0,1:T(4,128)(2,1)}), bf16[3,64,8192]{2,0,1:T(4,128)(2,1)}, u32[]{:S(2)}, u32[]{:S(2)}) async-start(bf16[3,64,8192]{2,0,1:T(4,128)(2,1)} %copy.15), calls=%async_computation | async-start | bytes 8388608 | tf_op jit(solution)/shard_map/all_to_all | solution.py:16
  21.6 6.4 %copy-start.2 = (f32[8192]{0:T(1024)S(1)}, f32[8192]{0:T(1024)}, u32[]{:S(2)}) copy-start(f32[8192]{0:T(1024)} %param.11) | copy-start | bytes 98308
  21.6 112.1 %all-gather.2.cloned.1.call-start = ((), (), s32[]{:S(2)}) async-start(), calls=%async_computation.2 | async-start | bytes 2162688 | tf_op jit(solution)/shard_map/all_gather | solution.py:24
  157.5 52.9 %all-to-all-start.1 = ((bf16[2,32,2,8192]{3,2,0,1:T(2,128)(2,1)}), bf16[2,32,2,8192]{3,2,0,1:T(2,128)(2,1)S(1)}, u32[]{:S(2)}, u32[]{:S(2)}) async-start(bf16[2,32,2,8192]{3,2,0,1:T(2,128)(2,1)} %copy.19), calls=%async_computation.1 | async-start | bytes 4194304 | tf_op jit(solution)/shard_map/all_to_all | solution.py:41
  210.4 4.1 %copy-start.1 = (bf16[256,8192]{1,0:T(8,128)(2,1)S(1)}, bf16[256,8192]{1,0:T(8,128)(2,1)}, u32[]{:S(2)}) copy-start(bf16[256,8192]{1,0:T(8,128)(2,1)} %param.13) | copy-start | bytes 12582916
Sparse Core Ops, SparseCore 0:
  32.7 79.4 all-gather.1
where the time goes:
time: 286 us
  waiting for transfers between devices  142 us (50%)
  blocking collectives  61.8 us (22%)
  local copies, waits for them, and re-layouts  30 us (10%)
  matrix products  25.6 us (9%)
  between operations  13.5 us (5%)
  starting transfers between devices  11.6 us (4%)
    all_to_all x1, waiting for transfers between devices, body(): lax.all_to_all(own_embed, 'dev', split_axis=1, concat_axis=0, tiled=True)  93.2 us
    unnamed x1, blocking collectives  61.8 us
    all_to_all x1, waiting for transfers between devices, body(): lax.all_to_all(spread, 'dev', split_axis=1, concat_axis=0, tiled=True)  48.7 us
    dot_general x1, matrix products, body(): jnp.einsum('vtd,dh->vth', grouped.astype(jnp.float32), keyq, precision=la...  8.99 us
    reshape x2, local copies, waits for them, and re-layouts, body(): spread = pooled.reshape(own_tokens, group_size, HEADS // group_size, D)  8.65 us
    all_to_all x1, local copies, waits for them, and re-layouts, body(): lax.all_to_all(own_embed, 'dev', split_axis=1, concat_axis=0, tiled=True)  7.92 us
    all_to_all x1, starting transfers between devices, body(): lax.all_to_all(own_embed, 'dev', split_axis=1, concat_axis=0, tiled=True)  7.44 us
    reshape x1, local copies, waits for them, and re-layouts, body(): key_w.astype(jnp.float32).reshape(key_rows, HEADS, HD)  6.36 us
  transfers between devices with their start and end apart: 3, of which 2 were waited for; matrix products, arithmetic and copies ran while one was open for 7% of the time, Pallas kernels for 0%

commit v1 on v0

--- a/solution.py
+++ b/solution.py
@@ -9,11 +9,18 @@
 V = 91
 
 
+def swap_blocks(shard, name, split, join):
+    size = lax.axis_size(name)
+    shards = jnp.stack(jnp.split(shard, size, axis=split), axis=0)
+    shards = lax.all_to_all(shards, name, split_axis=0, concat_axis=0)
+    return jnp.concatenate(shards, axis=join)
+
+
 def body(pixels, embed_w, var_embed, key_w, query, value_t, out_w):
     group_size = lax.axis_size("dev")
     own_embed = jnp.einsum("vtp,vpd->vtd", pixels, embed_w, preferred_element_type=jnp.float32)
     own_embed = (own_embed + var_embed.astype(jnp.float32)[:, None, :]).astype(jnp.bfloat16)
-    grouped = lax.all_to_all(own_embed, "dev", split_axis=1, concat_axis=0, tiled=True)
+    grouped = swap_blocks(own_embed, "dev", 1, 0)
     key_rows = key_w.shape[0]
     keyq_part = jnp.einsum(
         "dhj,hj->dh",

time: 286 us -> 275 us (0.962)
  waiting for transfers between devices: 142 us -> 120 us
  local copies, waits for them, and re-layouts: 30 us -> 40.7 us
    all_to_all x1, waiting for transfers between devices: 93.2 us -> 0.01 us  [swap_blocks(): shards = lax.all_to_all(shards, name, split_axis=0, concat_axis=0)]
    all_gather x1, waiting for transfers between devices: 0.01 us -> 71.1 us  [body(): keyq = lax.all_gather(keyq_part, 'dev', axis=0, tiled=True)]
    unnamed x6 -> x37, local copies, waits for them, and re-layouts: 0.24 us -> 22.7 us
    all_to_all x1 -> x0, local copies, waits for them, and re-layouts: 7.92 us -> none  [body(): lax.all_to_all(own_embed, 'dev', split_axis=1, concat_axis=0, tiled=True)]
    convert_element_type x1 -> x0, local copies, waits for them, and re-layouts: 4.67 us -> none  [body(): (own_embed + var_embed.astype(jnp.float32)[:, None, :]).astype(jnp.bfloat16)]
  transfers between devices with their start and end apart: 3 -> 3, of which waited for: 2 -> 2; matrix products, arithmetic and copies ran while one was open for 7% -> 4% of each run, Pallas kernels for 0% -> 0%
where the time goes in v1:
time: 275 us; the launch traced here: 274 us
  waiting for transfers between devices  120 us (44%)
  blocking collectives  61.8 us (22%)
  local copies, waits for them, and re-layouts  40.7 us (15%)
  matrix products  25.4 us (9%)
  between operations  13.5 us (5%)
  starting transfers between devices  12.1 us (4%)
    all_gather x1, waiting for transfers between devices, body(): keyq = lax.all_gather(keyq_part, 'dev', axis=0, tiled=True)  71.1 us
    unnamed x1, blocking collectives  61.8 us
    all_to_all x1, waiting for transfers between devices, body(): lax.all_to_all(spread, 'dev', split_axis=1, concat_axis=0, tiled=True)  48.7 us
    unnamed x37, local copies, waits for them, and re-layouts  22.7 us
    dot_general x1, matrix products, body(): jnp.einsum('vtd,dh->vth', grouped.astype(jnp.float32), keyq, precision=la...  8.99 us
    reshape x2, local copies, waits for them, and re-layouts, body(): spread = pooled.reshape(own_tokens, group_size, HEADS // group_size, D)  8.66 us
    all_to_all x1, starting transfers between devices, swap_blocks(): shards = lax.all_to_all(shards, name, split_axis=0, concat_axis=0)  7.43 us
    reshape x1, local copies, waits for them, and re-layouts, body(): key_w.astype(jnp.float32).reshape(key_rows, HEADS, HD)  6.4 us
  transfers between devices with their start and end apart: 3, of which 2 were waited for; matrix products, arithmetic and copies ran while one was open for 4% of the time, Pallas kernels for 0%

profile of v1, /device:TPU:0, one launch (start us, length us, event | category | flops | bytes accessed | tf_op | source)
XLA Modules:
  0.0 274.3 jit_solution(15570230848148376057)
XLA Ops:
  6.5 0.9 convert_element_type.26
  7.7 1.7 fusion.1
  11.6 0.7 fusion.54
  13.0 0.7 fusion.52
  14.5 0.7 fusion.50
  15.9 0.7 fusion.48
  16.6 0.8 fusion.47
  17.4 0.7 fusion.46
  18.8 0.7 fusion.44
  19.6 0.7 fusion.43
  23.2 0.7 fusion.38
  25.3 0.7 fusion.35
  26.1 0.7 fusion.34
  27.5 0.7 fusion.32
  28.3 0.7 fusion.31
  30.4 0.7 fusion.28
  31.1 0.7 fusion.27
  31.9 0.7 fusion.26
  32.6 7.4 %all-to-all-start = ((bf16[32,3,2,8192]{3,2,1,0:T(2,128)(2,1)}), bf16[32,3,2,8192]{3,2,1,0:T(2,128)(2,1)}, u32[]{:S(2)}, u32[]{:S(2)}) async-start(bf16[32,3,2,8192]{3,2,1,0:T(2,128)(2,1)} %fusion.26), calls=%async_computation | async-start | bytes 6291456 | tf_op jit(solution)/shard_map/all_to_all | solution.py:15
  40.3 6.4 %copy.23 = bf16[256,8192]{0,1:T(8,128)(2,1)} copy(bf16[256,8192]{1,0:T(8,128)(2,1)} %param.10) | data formatting | bytes 8388608 | tf_op jit(solution)/shard_map/reshape | solution.py:27
  46.7 3.9 %fusion.64 = f32[64,1,256]{2,1,0:T(1,128)S(1)} fusion(f32[64,128,1]{1,2,0:T(1,128)S(1)} %bitcast.171, bf16[256,64,128]{0,2,1:T(8,128)(2,1)} %bitcast.167), kind=kOutput, calls=%fused_computation.90 | convolution fusion | flops 25165824 | bytes 4292608 | tf_op jit(solution)/shard_map/dhj,hj->dh/dot_general | solution.py:25
  51.3 71.1 %all-gather.2.cloned.1.call-done = f32[8192,64]{0,1:T(8,128)} async-done(((f32[256,64]{0,1:T(8,128)}), f32[8192,64]{0,1:T(8,128)}) %all-gather.2.cloned.1.call-update) | async-done | bytes 2097168 | tf_op jit(solution)/shard_map/all_gather | solution.py:31
  122.3 9.0 %fusion.15 = f32[96,2,64]{0,2,1:T(8,128)S(1)} fusion(f32[8192,64]{0,1:T(8,128)} %all-gather.2.cloned.1.call-done, bf16[96,2,8192]{2,1,0:T(2,128)(2,1)} %bitcast.32, pred[96]{0:T(512)(128)(4,1)S(1)} %iota_compare_fusion), kind=kOutput, calls=%fused_computation.13 | convolution fusion | flops 1207984128 | bytes 5292128 | tf_op jit(solution)/shard_map/vtd,dh->vth/dot_general | solution.py:32
  131.5 5.8 %convolution_convert_fusion = bf16[2,64,8192]{2,1,0:T(8,128)(2,1)S(1)} fusion(bf16[96,2,8192]{2,1,0:T(2,128)(2,1)} %bitcast.32, f32[2,64]{1,0:T(2,128)S(1)} %fusion.63, f32[96,2,64]{0,2,1:T(8,128)S(1)} %fusion.15), kind=kOutput, calls=%fused_computation.3 | convolution fusion | flops 202412256 | bytes 5292544 | tf_op jit(solution)/shard_map/vth,vtd->thd/dot_general | solution.py:40
  137.3 2.7 reshape.27
  140.0 6.0 %copy.17 = bf16[2,32,2,8192]{3,2,0,1:T(2,128)(2,1)} copy(bf16[2,32,2,8192]{3,2,1,0:T(2,128)(2,1)} %reshape.27) | data formatting | bytes 4194304 | tf_op jit(solution)/shard_map/reshape | solution.py:47
  146.0 4.4 %all-to-all-start.1 = ((bf16[2,32,2,8192]{3,2,0,1:T(2,128)(2,1)}), bf16[2,32,2,8192]{3,2,0,1:T(2,128)(2,1)S(1)}, u32[]{:S(2)}, u32[]{:S(2)}) async-start(bf16[2,32,2,8192]{3,2,0,1:T(2,128)(2,1)} %copy.17), calls=%async_computation.1 | async-start | bytes 4194304 | tf_op jit(solution)/shard_map/all_to_all | solution.py:48
  150.4 48.7 %all-to-all-done.1 = bf16[2,32,2,8192]{3,2,0,1:T(2,128)(2,1)S(1)} async-done(((bf16[2,32,2,8192]{3,2,0,1:T(2,128)(2,1)}), bf16[2,32,2,8192]{3,2,0,1:T(2,128)(2,1)S(1)}, u32[]{:S(2)}, u32[]{:S(2)}) %all-to-all-start.1) | async-done | bytes 2097184 | tf_op jit(solution)/shard_map/all_to_all | solution.py:48
  199.1 4.1 %fusion.23 = bf16[2,8,8,128]{3,2,1,0:T(8,128)(2,1)S(1)} fusion(bf16[2,128,8192]{2,1,0:T(8,128)(2,1)} %bitcast.169, bf16[64,2,8192]{2,1,0:T(2,128)(2,1)S(1)} %bitcast.168), kind=kOutput, calls=%fused_computation.15 | convolution fusion | flops 268451840 | bytes 6324224 | tf_op jit(solution)/shard_map/thd,hcd->thc/dot_general | solution.py:53
  203.2 0.8 fusion.58
  204.1 61.8 %all-reduce.2 = bf16[64,8192]{1,0:T(8,128)(2,1)} all-reduce(f32[64,8192]{1,0:T(8,128)S(1)} %fusion.58), channel_id=2, replica_groups=mesh['dev'=32] {'dev'}, use_global_device_ids=true, to_apply=%region_2.3.clone | all-reduce | flops 524288 | bytes 3145728
  265.9 1.6 dynamic-slice_convert_fusion
  (28 shorter events, 12.7 us)
Async XLA Ops:
  6.5 1.2 copy-start
  32.6 89.7 %all-to-all-start = ((bf16[32,3,2,8192]{3,2,1,0:T(2,128)(2,1)}), bf16[32,3,2,8192]{3,2,1,0:T(2,128)(2,1)}, u32[]{:S(2)}, u32[]{:S(2)}) async-start(bf16[32,3,2,8192]{3,2,1,0:T(2,128)(2,1)} %fusion.26), calls=%async_computation | async-start | bytes 6291456 | tf_op jit(solution)/shard_map/all_to_all | solution.py:15
  40.1 6.6 %copy-start.2 = (f32[8192]{0:T(1024)S(1)}, f32[8192]{0:T(1024)}, u32[]{:S(2)}) copy-start(f32[8192]{0:T(1024)} %param.11) | copy-start | bytes 98308
  40.1 82.3 %all-gather.2.cloned.1.call-start = ((), (), s32[]{:S(2)}) async-start(), calls=%async_computation.2 | async-start | bytes 2162688 | tf_op jit(solution)/shard_map/all_gather | solution.py:31
  146.0 53.1 %all-to-all-start.1 = ((bf16[2,32,2,8192]{3,2,0,1:T(2,128)(2,1)}), bf16[2,32,2,8192]{3,2,0,1:T(2,128)(2,1)S(1)}, u32[]{:S(2)}, u32[]{:S(2)}) async-start(bf16[2,32,2,8192]{3,2,0,1:T(2,128)(2,1)} %copy.17), calls=%async_computation.1 | async-start | bytes 4194304 | tf_op jit(solution)/shard_map/all_to_all | solution.py:48
  199.1 4.1 %copy-start.1 = (bf16[256,8192]{1,0:T(8,128)(2,1)S(1)}, bf16[256,8192]{1,0:T(8,128)(2,1)}, u32[]{:S(2)}) copy-start(bf16[256,8192]{1,0:T(8,128)(2,1)} %param.13) | copy-start | bytes 12582916
Sparse Core Ops, SparseCore 0:
  51.4 70.9 all-gather.1
